TPU v7x, 32 devices: a 4x4x1 block of a 4x4x8 slice. The times are simulated.
32 devices in a mesh: data: 1 (over z), time: 32 (over y, x, core).
Axes of the slice: x: 4, y: 4, z: 1, core: 2. Of those that a mesh axis runs over, the one named last changes fastest.
The devices are a block of a 4x4x8 slice.
Arguments:
- x_init: float32 [4, 256, 1152], P('data')
- w_in: bfloat16 [1152, 4608], replicated
- w_out: bfloat16 [4608, 1152], replicated
- gamma_c: bfloat16 [64, 4608], P('time')
- beta_c: bfloat16 [64, 4608], P('time')
- gamma_u: bfloat16 [64, 4608], P('time')
- beta_u: bfloat16 [64, 4608], P('time')
- step_h: float32 [64], P('time')
- guide_w: float32 [1], replicated
Outputs:
- output: float32 [64, 4, 256, 1152], P('time', 'data')
All inputs are finite; a program needn't handle non-finite values.
Results may differ from a plain program's by a relative error of at most 0.00983.
Values are sent between devices in bfloat16 or wider.
A program may use at most 768 MiB of HBM per device.

v0:
```python
import jax
import jax.numpy as jnp
import math
from jax import lax
from jax.sharding import PartitionSpec as P

NUM_SWEEPS = 4


def solution(mesh):
    num_time = mesh.shape["time"]
    num_levels = math.ceil(math.log2(num_time))
    shift_perms = [[(src, src + 2 ** level) for src in range(num_time - 2 ** level)] for level in range(num_levels)]

    def local(x_init, w_in, w_out, gamma_c, beta_c, gamma_u, beta_u, step_h, guide_w):
        guide = guide_w[0]
        gain_pair = 1.0 + jnp.stack([gamma_c, gamma_u], axis=0).astype(jnp.float32)
        shift_pair = jnp.stack([beta_c, beta_u], axis=0).astype(jnp.float32)

        def sweep(index, states):
            pre_act = jnp.einsum("kbnc,cd->kbnd", states.astype(jnp.bfloat16), w_in, preferred_element_type=jnp.float32)
            act = jax.nn.gelu(pre_act[None] * gain_pair[:, :, None, None, :] + shift_pair[:, :, None, None, :]).astype(jnp.bfloat16)
            outs = jnp.einsum("ekbnd,dc->ekbnc", act, w_out, preferred_element_type=jnp.float32)
            drift = step_h[:, None, None, None] * ((1.0 + guide) * outs[0] - guide * outs[1])
            running = jnp.cumsum(drift, axis=0)
            dev_total = running[-1]
            prefix = dev_total
            for perm in shift_perms:
                prefix = prefix + lax.ppermute(prefix, "time", perm)
            before = prefix - dev_total
            local_before = jnp.concatenate([jnp.zeros_like(drift[:1]), running[:-1]], axis=0)
            return x_init[None] + (before[None] + local_before)

        start = jnp.broadcast_to(x_init[None], (step_h.shape[0],) + x_init.shape)
        return lax.fori_loop(0, NUM_SWEEPS, sweep, start)

    return jax.shard_map(local, mesh=mesh, in_specs=(P("data", None, None), P(None, None), P(None, None), P("time", None), P("time", None), P("time", None), P("time", None), P("time"), P(None)), out_specs=P("time", "data", None, None), check_vma=False)
```

profile of v0, /device:TPU:97, one launch (start us, length us, event | category | flops | bytes accessed | tf_op | source)
XLA Modules:
  0.0 2475.3 jit_solution(10624392336504588764)
XLA Ops:
  8.9 2466.4 %while.11 = (s32[]{:T(128)}, f32[2,4,256,1152]{3,2,1,0:T(8,128)}, f32[4,256,1152]{2,1,0:T(8,128)}, f32[2]{0:T(128)}, f32[]{:T(128)}, /*index=5*/bf16[1152,4608]{...) while((s32[]{:T(128)}, f32[2,4,256,1152]{3,2,1,0:T(8,128)}, ...), condition=%wide.region_2.3_spmd, body=%wide.region_0.2_spmd.sunk | while | flops 65463386112 | bytes 403587456 | solution.py:35
  41.5 77.0 %fusion.52 = f32[2,2,4,256,1152]{4,3,2,1,0:T(8,128)} fusion(f32[2,2,4608]{2,1,0:T(2,128)S(1)} %get-tuple-element.210, f32[2,2,4608]{2,1,0:T(2,128)S(1)} %get-tuple-element.209, f32[2,4,256,4608]{3,2,1,0:T(8,128)} %fusion.51, bf16[4608,1152]{1,0:T(8,128)(2,1)} %get-tuple-element.211), kind=kOutput, calls=%fused_computation.9.clone.2 | convolution fusion | flops 43694161920 | bytes 67387392 | tf_op jit(solution)/shard_map/while/body/eval_jaxpr/ekbnd,dc->ekbnc/dot_general | solution.py:23
  134.2 51.0 %collective-permute-done = f32[4,256,1152]{2,1,0:T(8,128)S(1)} collective-permute-done((f32[4,256,1152]{2,1,0:T(8,128)S(1)}, f32[4,256,1152]{2,1,0:T(8,128)S(1)}, u32[]{:S(2)}, u32[]{:S(2)}) %collective-permute-start) | collective-permute-done | bytes 4718624 | tf_op jit(solution)/shard_map/while/body/eval_jaxpr/ppermute | solution.py:29
  189.4 99.6 %collective-permute-done.1 = f32[4,256,1152]{2,1,0:T(8,128)S(1)} collective-permute-done((f32[4,256,1152]{2,1,0:T(8,128)S(1)}, f32[4,256,1152]{2,1,0:T(8,128)S(1)}, u32[]{:S(2)}, u32[]{:S(2)}) %collective-permute-start.1) | collective-permute-done | bytes 4718624 | tf_op jit(solution)/shard_map/while/body/eval_jaxpr/ppermute | solution.py:29
  295.0 98.4 %collective-permute-done.2 = f32[4,256,1152]{2,1,0:T(8,128)S(1)} collective-permute-done((f32[4,256,1152]{2,1,0:T(8,128)S(1)}, f32[4,256,1152]{2,1,0:T(8,128)S(1)}, u32[]{:S(2)}, u32[]{:S(2)}) %collective-permute-start.2) | collective-permute-done | bytes 4718624 | tf_op jit(solution)/shard_map/while/body/eval_jaxpr/ppermute | solution.py:29
  398.1 95.0 %collective-permute-done.3 = f32[4,256,1152]{2,1,0:T(8,128)S(1)} collective-permute-done((f32[4,256,1152]{2,1,0:T(8,128)S(1)}, f32[4,256,1152]{2,1,0:T(8,128)S(1)}, u32[]{:S(2)}, u32[]{:S(2)}) %collective-permute-start.3) | collective-permute-done | bytes 4718624 | tf_op jit(solution)/shard_map/while/body/eval_jaxpr/ppermute | solution.py:29
  504.3 92.3 %collective-permute-done.4 = f32[4,256,1152]{2,1,0:T(8,128)} collective-permute-done((f32[4,256,1152]{2,1,0:T(8,128)}, f32[4,256,1152]{2,1,0:T(8,128)}, u32[]{:S(2)}, u32[]{:S(2)}) %collective-permute-start.4) | collective-permute-done | bytes 4718624 | tf_op jit(solution)/shard_map/while/body/eval_jaxpr/ppermute | solution.py:29
  646.8 77.0 %fusion.52 = f32[2,2,4,256,1152]{4,3,2,1,0:T(8,128)} fusion(f32[2,2,4608]{2,1,0:T(2,128)S(1)} %get-tuple-element.210, f32[2,2,4608]{2,1,0:T(2,128)S(1)} %get-tuple-element.209, f32[2,4,256,4608]{3,2,1,0:T(8,128)} %fusion.51, bf16[4608,1152]{1,0:T(8,128)(2,1)} %get-tuple-element.211), kind=kOutput, calls=%fused_computation.9.clone.2 | convolution fusion | flops 43694161920 | bytes 67387392 | tf_op jit(solution)/shard_map/while/body/eval_jaxpr/ekbnd,dc->ekbnc/dot_general | solution.py:23
  749.0 51.0 %collective-permute-done = f32[4,256,1152]{2,1,0:T(8,128)S(1)} collective-permute-done((f32[4,256,1152]{2,1,0:T(8,128)S(1)}, f32[4,256,1152]{2,1,0:T(8,128)S(1)}, u32[]{:S(2)}, u32[]{:S(2)}) %collective-permute-start) | collective-permute-done | bytes 4718624 | tf_op jit(solution)/shard_map/while/body/eval_jaxpr/ppermute | solution.py:29
  803.8 99.2 %collective-permute-done.1 = f32[4,256,1152]{2,1,0:T(8,128)S(1)} collective-permute-done((f32[4,256,1152]{2,1,0:T(8,128)S(1)}, f32[4,256,1152]{2,1,0:T(8,128)S(1)}, u32[]{:S(2)}, u32[]{:S(2)}) %collective-permute-start.1) | collective-permute-done | bytes 4718624 | tf_op jit(solution)/shard_map/while/body/eval_jaxpr/ppermute | solution.py:29
  909.4 98.4 %collective-permute-done.2 = f32[4,256,1152]{2,1,0:T(8,128)S(1)} collective-permute-done((f32[4,256,1152]{2,1,0:T(8,128)S(1)}, f32[4,256,1152]{2,1,0:T(8,128)S(1)}, u32[]{:S(2)}, u32[]{:S(2)}) %collective-permute-start.2) | collective-permute-done | bytes 4718624 | tf_op jit(solution)/shard_map/while/body/eval_jaxpr/ppermute | solution.py:29
  1018.3 98.2 %collective-permute-done.3 = f32[4,256,1152]{2,1,0:T(8,128)S(1)} collective-permute-done((f32[4,256,1152]{2,1,0:T(8,128)S(1)}, f32[4,256,1152]{2,1,0:T(8,128)S(1)}, u32[]{:S(2)}, u32[]{:S(2)}) %collective-permute-start.3) | collective-permute-done | bytes 4718624 | tf_op jit(solution)/shard_map/while/body/eval_jaxpr/ppermute | solution.py:29
  1128.3 95.5 %collective-permute-done.4 = f32[4,256,1152]{2,1,0:T(8,128)} collective-permute-done((f32[4,256,1152]{2,1,0:T(8,128)}, f32[4,256,1152]{2,1,0:T(8,128)}, u32[]{:S(2)}, u32[]{:S(2)}) %collective-permute-start.4) | collective-permute-done | bytes 4718624 | tf_op jit(solution)/shard_map/while/body/eval_jaxpr/ppermute | solution.py:29
  1274.0 77.0 %fusion.52 = f32[2,2,4,256,1152]{4,3,2,1,0:T(8,128)} fusion(f32[2,2,4608]{2,1,0:T(2,128)S(1)} %get-tuple-element.210, f32[2,2,4608]{2,1,0:T(2,128)S(1)} %get-tuple-element.209, f32[2,4,256,4608]{3,2,1,0:T(8,128)} %fusion.51, bf16[4608,1152]{1,0:T(8,128)(2,1)} %get-tuple-element.211), kind=kOutput, calls=%fused_computation.9.clone.2 | convolution fusion | flops 43694161920 | bytes 67387392 | tf_op jit(solution)/shard_map/while/body/eval_jaxpr/ekbnd,dc->ekbnc/dot_general | solution.py:23
  1364.0 51.0 %collective-permute-done = f32[4,256,1152]{2,1,0:T(8,128)S(1)} collective-permute-done((f32[4,256,1152]{2,1,0:T(8,128)S(1)}, f32[4,256,1152]{2,1,0:T(8,128)S(1)}, u32[]{:S(2)}, u32[]{:S(2)}) %collective-permute-start) | collective-permute-done | bytes 4718624 | tf_op jit(solution)/shard_map/while/body/eval_jaxpr/ppermute | solution.py:29
  1421.6 100.6 %collective-permute-done.1 = f32[4,256,1152]{2,1,0:T(8,128)S(1)} collective-permute-done((f32[4,256,1152]{2,1,0:T(8,128)S(1)}, f32[4,256,1152]{2,1,0:T(8,128)S(1)}, u32[]{:S(2)}, u32[]{:S(2)}) %collective-permute-start.1) | collective-permute-done | bytes 4718624 | tf_op jit(solution)/shard_map/while/body/eval_jaxpr/ppermute | solution.py:29
  1529.5 101.3 %collective-permute-done.2 = f32[4,256,1152]{2,1,0:T(8,128)S(1)} collective-permute-done((f32[4,256,1152]{2,1,0:T(8,128)S(1)}, f32[4,256,1152]{2,1,0:T(8,128)S(1)}, u32[]{:S(2)}, u32[]{:S(2)}) %collective-permute-start.2) | collective-permute-done | bytes 4718624 | tf_op jit(solution)/shard_map/while/body/eval_jaxpr/ppermute | solution.py:29
  1632.9 97.4 %collective-permute-done.3 = f32[4,256,1152]{2,1,0:T(8,128)S(1)} collective-permute-done((f32[4,256,1152]{2,1,0:T(8,128)S(1)}, f32[4,256,1152]{2,1,0:T(8,128)S(1)}, u32[]{:S(2)}, u32[]{:S(2)}) %collective-permute-start.3) | collective-permute-done | bytes 4718624 | tf_op jit(solution)/shard_map/while/body/eval_jaxpr/ppermute | solution.py:29
  1741.8 94.7 %collective-permute-done.4 = f32[4,256,1152]{2,1,0:T(8,128)} collective-permute-done((f32[4,256,1152]{2,1,0:T(8,128)}, f32[4,256,1152]{2,1,0:T(8,128)}, u32[]{:S(2)}, u32[]{:S(2)}) %collective-permute-start.4) | collective-permute-done | bytes 4718624 | tf_op jit(solution)/shard_map/while/body/eval_jaxpr/ppermute | solution.py:29
  1886.7 77.0 %fusion.52 = f32[2,2,4,256,1152]{4,3,2,1,0:T(8,128)} fusion(f32[2,2,4608]{2,1,0:T(2,128)S(1)} %get-tuple-element.210, f32[2,2,4608]{2,1,0:T(2,128)S(1)} %get-tuple-element.209, f32[2,4,256,4608]{3,2,1,0:T(8,128)} %fusion.51, bf16[4608,1152]{1,0:T(8,128)(2,1)} %get-tuple-element.211), kind=kOutput, calls=%fused_computation.9.clone.2 | convolution fusion | flops 43694161920 | bytes 67387392 | tf_op jit(solution)/shard_map/while/body/eval_jaxpr/ekbnd,dc->ekbnc/dot_general | solution.py:23
  2040.0 98.6 %collective-permute-done.1 = f32[4,256,1152]{2,1,0:T(8,128)S(1)} collective-permute-done((f32[4,256,1152]{2,1,0:T(8,128)S(1)}, f32[4,256,1152]{2,1,0:T(8,128)S(1)}, u32[]{:S(2)}, u32[]{:S(2)}) %collective-permute-start.1) | collective-permute-done | bytes 4718624 | tf_op jit(solution)/shard_map/while/body/eval_jaxpr/ppermute | solution.py:29
  2149.3 100.7 %collective-permute-done.2 = f32[4,256,1152]{2,1,0:T(8,128)S(1)} collective-permute-done((f32[4,256,1152]{2,1,0:T(8,128)S(1)}, f32[4,256,1152]{2,1,0:T(8,128)S(1)}, u32[]{:S(2)}, u32[]{:S(2)}) %collective-permute-start.2) | collective-permute-done | bytes 4718624 | tf_op jit(solution)/shard_map/while/body/eval_jaxpr/ppermute | solution.py:29
  2254.3 99.0 %collective-permute-done.3 = f32[4,256,1152]{2,1,0:T(8,128)S(1)} collective-permute-done((f32[4,256,1152]{2,1,0:T(8,128)S(1)}, f32[4,256,1152]{2,1,0:T(8,128)S(1)}, u32[]{:S(2)}, u32[]{:S(2)}) %collective-permute-start.3) | collective-permute-done | bytes 4718624 | tf_op jit(solution)/shard_map/while/body/eval_jaxpr/ppermute | solution.py:29
  2363.0 94.8 %collective-permute-done.4 = f32[4,256,1152]{2,1,0:T(8,128)} collective-permute-done((f32[4,256,1152]{2,1,0:T(8,128)}, f32[4,256,1152]{2,1,0:T(8,128)}, u32[]{:S(2)}, u32[]{:S(2)}) %collective-permute-start.4) | collective-permute-done | bytes 4718624 | tf_op jit(solution)/shard_map/while/body/eval_jaxpr/ppermute | solution.py:29
  (76 shorter events, 449.4 us)
Async XLA Ops:
  41.5 77.0 %copy-start.1 = (f32[2]{0:T(128)S(1)}, f32[2]{0:T(128)}, u32[]{:S(2)}) copy-start(f32[2]{0:T(128)} %get-tuple-element.206) | copy-start | bytes 28 | tf_op jit(solution)/shard_map/while
  129.6 55.6 %collective-permute-start = (f32[4,256,1152]{2,1,0:T(8,128)S(1)}, f32[4,256,1152]{2,1,0:T(8,128)S(1)}, u32[]{:S(2)}, u32[]{:S(2)}) collective-permute-start(f32[4,256,1152]{2,1,0:T(8,128)S(1)} %get-tuple-element.180), channel_id=1, source_target_pairs={{0,1},{1,2},{2,3},{3,4},{4,5},{5,6},{6,7},{7,8},{8,9},{9,10},{10,1... | collective-permute-start | bytes 14155784 | tf_op jit(solution)/shard_map/while/body/eval_jaxpr/ppermute | solution.py:29
  185.8 103.2 %collective-permute-start.1 = (f32[4,256,1152]{2,1,0:T(8,128)S(1)}, f32[4,256,1152]{2,1,0:T(8,128)S(1)}, u32[]{:S(2)}, u32[]{:S(2)}) collective-permute-start(f32[4,256,1152]{2,1,0:T(8,128)S(1)} %fusion.54), channel_id=1, source_target_pairs={{0,2},{1,3},{2,4},{3,5},{4,6},{5,7},{6,8},{7,9},{8,10},{9,11},{10,... | collective-permute-start | bytes 14155784 | tf_op jit(solution)/shard_map/while/body/eval_jaxpr/ppermute | solution.py:29
  289.4 103.9 %collective-permute-start.2 = (f32[4,256,1152]{2,1,0:T(8,128)S(1)}, f32[4,256,1152]{2,1,0:T(8,128)S(1)}, u32[]{:S(2)}, u32[]{:S(2)}) collective-permute-start(f32[4,256,1152]{2,1,0:T(8,128)S(1)} %add.147), channel_id=1, source_target_pairs={{0,4},{1,5},{2,6},{3,7},{4,8},{5,9},{6,10},{7,11},{8,12},{9,13},{1... | collective-permute-start | bytes 14155784 | tf_op jit(solution)/shard_map/while/body/eval_jaxpr/ppermute | solution.py:29
  393.9 99.2 %collective-permute-start.3 = (f32[4,256,1152]{2,1,0:T(8,128)S(1)}, f32[4,256,1152]{2,1,0:T(8,128)S(1)}, u32[]{:S(2)}, u32[]{:S(2)}) collective-permute-start(f32[4,256,1152]{2,1,0:T(8,128)S(1)} %add.148), channel_id=1, source_target_pairs={{0,8},{1,9},{2,10},{3,11},{4,12},{5,13},{6,14},{7,15},{8,16},{9,17... | collective-permute-start | bytes 14155784 | tf_op jit(solution)/shard_map/while/body/eval_jaxpr/ppermute | solution.py:29
  495.8 100.8 %collective-permute-start.4 = (f32[4,256,1152]{2,1,0:T(8,128)}, f32[4,256,1152]{2,1,0:T(8,128)}, u32[]{:S(2)}, u32[]{:S(2)}) collective-permute-start(f32[4,256,1152]{2,1,0:T(8,128)} %add.149), channel_id=1, source_target_pairs={{0,16},{1,17},{2,18},{3,19},{4,20},{5,21},{6,22},{7,23},{8,24},{9,... | collective-permute-start | bytes 14155784 | tf_op jit(solution)/shard_map/while/body/eval_jaxpr/ppermute | solution.py:29
  646.8 77.0 %copy-start.1 = (f32[2]{0:T(128)S(1)}, f32[2]{0:T(128)}, u32[]{:S(2)}) copy-start(f32[2]{0:T(128)} %get-tuple-element.206) | copy-start | bytes 28 | tf_op jit(solution)/shard_map/while
  734.9 65.1 %collective-permute-start = (f32[4,256,1152]{2,1,0:T(8,128)S(1)}, f32[4,256,1152]{2,1,0:T(8,128)S(1)}, u32[]{:S(2)}, u32[]{:S(2)}) collective-permute-start(f32[4,256,1152]{2,1,0:T(8,128)S(1)} %get-tuple-element.180), channel_id=1, source_target_pairs={{0,1},{1,2},{2,3},{3,4},{4,5},{5,6},{6,7},{7,8},{8,9},{9,10},{10,1... | collective-permute-start | bytes 14155784 | tf_op jit(solution)/shard_map/while/body/eval_jaxpr/ppermute | solution.py:29
  800.6 102.5 %collective-permute-start.1 = (f32[4,256,1152]{2,1,0:T(8,128)S(1)}, f32[4,256,1152]{2,1,0:T(8,128)S(1)}, u32[]{:S(2)}, u32[]{:S(2)}) collective-permute-start(f32[4,256,1152]{2,1,0:T(8,128)S(1)} %fusion.54), channel_id=1, source_target_pairs={{0,2},{1,3},{2,4},{3,5},{4,6},{5,7},{6,8},{7,9},{8,10},{9,11},{10,... | collective-permute-start | bytes 14155784 | tf_op jit(solution)/shard_map/while/body/eval_jaxpr/ppermute | solution.py:29
  903.5 104.3 %collective-permute-start.2 = (f32[4,256,1152]{2,1,0:T(8,128)S(1)}, f32[4,256,1152]{2,1,0:T(8,128)S(1)}, u32[]{:S(2)}, u32[]{:S(2)}) collective-permute-start(f32[4,256,1152]{2,1,0:T(8,128)S(1)} %add.147), channel_id=1, source_target_pairs={{0,4},{1,5},{2,6},{3,7},{4,8},{5,9},{6,10},{7,11},{8,12},{9,13},{1... | collective-permute-start | bytes 14155784 | tf_op jit(solution)/shard_map/while/body/eval_jaxpr/ppermute | solution.py:29
  1008.3 108.3 %collective-permute-start.3 = (f32[4,256,1152]{2,1,0:T(8,128)S(1)}, f32[4,256,1152]{2,1,0:T(8,128)S(1)}, u32[]{:S(2)}, u32[]{:S(2)}) collective-permute-start(f32[4,256,1152]{2,1,0:T(8,128)S(1)} %add.148), channel_id=1, source_target_pairs={{0,8},{1,9},{2,10},{3,11},{4,12},{5,13},{6,14},{7,15},{8,16},{9,17... | collective-permute-start | bytes 14155784 | tf_op jit(solution)/shard_map/while/body/eval_jaxpr/ppermute | solution.py:29
  1119.3 104.5 %collective-permute-start.4 = (f32[4,256,1152]{2,1,0:T(8,128)}, f32[4,256,1152]{2,1,0:T(8,128)}, u32[]{:S(2)}, u32[]{:S(2)}) collective-permute-start(f32[4,256,1152]{2,1,0:T(8,128)} %add.149), channel_id=1, source_target_pairs={{0,16},{1,17},{2,18},{3,19},{4,20},{5,21},{6,22},{7,23},{8,24},{9,... | collective-permute-start | bytes 14155784 | tf_op jit(solution)/shard_map/while/body/eval_jaxpr/ppermute | solution.py:29
  1274.0 77.0 %copy-start.1 = (f32[2]{0:T(128)S(1)}, f32[2]{0:T(128)}, u32[]{:S(2)}) copy-start(f32[2]{0:T(128)} %get-tuple-element.206) | copy-start | bytes 28 | tf_op jit(solution)/shard_map/while
  1362.1 53.0 %collective-permute-start = (f32[4,256,1152]{2,1,0:T(8,128)S(1)}, f32[4,256,1152]{2,1,0:T(8,128)S(1)}, u32[]{:S(2)}, u32[]{:S(2)}) collective-permute-start(f32[4,256,1152]{2,1,0:T(8,128)S(1)} %get-tuple-element.180), channel_id=1, source_target_pairs={{0,1},{1,2},{2,3},{3,4},{4,5},{5,6},{6,7},{7,8},{8,9},{9,10},{10,1... | collective-permute-start | bytes 14155784 | tf_op jit(solution)/shard_map/while/body/eval_jaxpr/ppermute | solution.py:29
  1415.6 106.6 %collective-permute-start.1 = (f32[4,256,1152]{2,1,0:T(8,128)S(1)}, f32[4,256,1152]{2,1,0:T(8,128)S(1)}, u32[]{:S(2)}, u32[]{:S(2)}) collective-permute-start(f32[4,256,1152]{2,1,0:T(8,128)S(1)} %fusion.54), channel_id=1, source_target_pairs={{0,2},{1,3},{2,4},{3,5},{4,6},{5,7},{6,8},{7,9},{8,10},{9,11},{10,... | collective-permute-start | bytes 14155784 | tf_op jit(solution)/shard_map/while/body/eval_jaxpr/ppermute | solution.py:29
  1522.7 108.1 %collective-permute-start.2 = (f32[4,256,1152]{2,1,0:T(8,128)S(1)}, f32[4,256,1152]{2,1,0:T(8,128)S(1)}, u32[]{:S(2)}, u32[]{:S(2)}) collective-permute-start(f32[4,256,1152]{2,1,0:T(8,128)S(1)} %add.147), channel_id=1, source_target_pairs={{0,4},{1,5},{2,6},{3,7},{4,8},{5,9},{6,10},{7,11},{8,12},{9,13},{1... | collective-permute-start | bytes 14155784 | tf_op jit(solution)/shard_map/while/body/eval_jaxpr/ppermute | solution.py:29
  1631.3 99.0 %collective-permute-start.3 = (f32[4,256,1152]{2,1,0:T(8,128)S(1)}, f32[4,256,1152]{2,1,0:T(8,128)S(1)}, u32[]{:S(2)}, u32[]{:S(2)}) collective-permute-start(f32[4,256,1152]{2,1,0:T(8,128)S(1)} %add.148), channel_id=1, source_target_pairs={{0,8},{1,9},{2,10},{3,11},{4,12},{5,13},{6,14},{7,15},{8,16},{9,17... | collective-permute-start | bytes 14155784 | tf_op jit(solution)/shard_map/while/body/eval_jaxpr/ppermute | solution.py:29
  1733.0 103.6 %collective-permute-start.4 = (f32[4,256,1152]{2,1,0:T(8,128)}, f32[4,256,1152]{2,1,0:T(8,128)}, u32[]{:S(2)}, u32[]{:S(2)}) collective-permute-start(f32[4,256,1152]{2,1,0:T(8,128)} %add.149), channel_id=1, source_target_pairs={{0,16},{1,17},{2,18},{3,19},{4,20},{5,21},{6,22},{7,23},{8,24},{9,... | collective-permute-start | bytes 14155784 | tf_op jit(solution)/shard_map/while/body/eval_jaxpr/ppermute | solution.py:29
  1886.7 77.0 %copy-start.1 = (f32[2]{0:T(128)S(1)}, f32[2]{0:T(128)}, u32[]{:S(2)}) copy-start(f32[2]{0:T(128)} %get-tuple-element.206) | copy-start | bytes 28 | tf_op jit(solution)/shard_map/while
  1974.8 61.9 %collective-permute-start = (f32[4,256,1152]{2,1,0:T(8,128)S(1)}, f32[4,256,1152]{2,1,0:T(8,128)S(1)}, u32[]{:S(2)}, u32[]{:S(2)}) collective-permute-start(f32[4,256,1152]{2,1,0:T(8,128)S(1)} %get-tuple-element.180), channel_id=1, source_target_pairs={{0,1},{1,2},{2,3},{3,4},{4,5},{5,6},{6,7},{7,8},{8,9},{9,10},{10,1... | collective-permute-start | bytes 14155784 | tf_op jit(solution)/shard_map/while/body/eval_jaxpr/ppermute | solution.py:29
  2037.4 101.3 %collective-permute-start.1 = (f32[4,256,1152]{2,1,0:T(8,128)S(1)}, f32[4,256,1152]{2,1,0:T(8,128)S(1)}, u32[]{:S(2)}, u32[]{:S(2)}) collective-permute-start(f32[4,256,1152]{2,1,0:T(8,128)S(1)} %fusion.54), channel_id=1, source_target_pairs={{0,2},{1,3},{2,4},{3,5},{4,6},{5,7},{6,8},{7,9},{8,10},{9,11},{10,... | collective-permute-start | bytes 14155784 | tf_op jit(solution)/shard_map/while/body/eval_jaxpr/ppermute | solution.py:29
  2139.1 110.9 %collective-permute-start.2 = (f32[4,256,1152]{2,1,0:T(8,128)S(1)}, f32[4,256,1152]{2,1,0:T(8,128)S(1)}, u32[]{:S(2)}, u32[]{:S(2)}) collective-permute-start(f32[4,256,1152]{2,1,0:T(8,128)S(1)} %add.147), channel_id=1, source_target_pairs={{0,4},{1,5},{2,6},{3,7},{4,8},{5,9},{6,10},{7,11},{8,12},{9,13},{1... | collective-permute-start | bytes 14155784 | tf_op jit(solution)/shard_map/while/body/eval_jaxpr/ppermute | solution.py:29
  2250.5 102.9 %collective-permute-start.3 = (f32[4,256,1152]{2,1,0:T(8,128)S(1)}, f32[4,256,1152]{2,1,0:T(8,128)S(1)}, u32[]{:S(2)}, u32[]{:S(2)}) collective-permute-start(f32[4,256,1152]{2,1,0:T(8,128)S(1)} %add.148), channel_id=1, source_target_pairs={{0,8},{1,9},{2,10},{3,11},{4,12},{5,13},{6,14},{7,15},{8,16},{9,17... | collective-permute-start | bytes 14155784 | tf_op jit(solution)/shard_map/while/body/eval_jaxpr/ppermute | solution.py:29
  2356.0 101.7 %collective-permute-start.4 = (f32[4,256,1152]{2,1,0:T(8,128)}, f32[4,256,1152]{2,1,0:T(8,128)}, u32[]{:S(2)}, u32[]{:S(2)}) collective-permute-start(f32[4,256,1152]{2,1,0:T(8,128)} %add.149), channel_id=1, source_target_pairs={{0,16},{1,17},{2,18},{3,19},{4,20},{5,21},{6,22},{7,23},{8,24},{9,... | collective-permute-start | bytes 14155784 | tf_op jit(solution)/shard_map/while/body/eval_jaxpr/ppermute | solution.py:29
  (4 other events, 248.0 us)
where the time goes:
time: 2480 us
  waiting for transfers between devices  1770 us (71%)
  matrix products  439 us (18%)
  starting transfers between devices  128 us (5%)
  other arithmetic  120 us (5%)
    ppermute x20, waiting for transfers between devices, sweep(): prefix = prefix + lax.ppermute(prefix, 'time', perm)  1770 us
    dot_general x4, matrix products, sweep(): jnp.einsum('ekbnd,dc->ekbnc', act, w_out, preferred_element_type=jnp.floa...  308 us
    dot_general x4, matrix products, sweep(): jnp.einsum('kbnc,cd->kbnd', states.astype(jnp.bfloat16), w_in, preferred_...  130 us
    ppermute x20, starting transfers between devices, sweep(): prefix = prefix + lax.ppermute(prefix, 'time', perm)  128 us
  transfers between devices with their start and end apart: 20, of which 20 were waited for; matrix products, arithmetic and copies ran while one was open for 0% of the time, Pallas kernels for 0%

commit v1 on v0

v1 whole, which is shorter than its diff:
```python
import jax
import jax.numpy as jnp
from jax import lax
from jax.sharding import PartitionSpec as P

NUM_SWEEPS = 4


def solution(mesh):
    num_time = mesh.shape["time"]

    def local(x_init, w_in, w_out, gamma_c, beta_c, gamma_u, beta_u, step_h, guide_w):
        samples, tokens, channels = x_init.shape
        own_steps, hidden = gamma_c.shape
        steps = own_steps * num_time
        total_rows = samples * tokens
        rows = total_rows // num_time
        guide = guide_w[0]

        mods = jnp.stack([gamma_c, beta_c, gamma_u, beta_u], axis=1)
        mods = lax.all_gather(mods, "time", axis=0, tiled=True).astype(jnp.float32)
        gains = (1.0 + mods[:, 0], 1.0 + mods[:, 2])
        shifts = (mods[:, 1], mods[:, 3])
        h_all = lax.all_gather(step_h, "time", axis=0, tiled=True)

        me = lax.axis_index("time")
        x_rows = lax.dynamic_slice_in_dim(x_init.reshape(total_rows, channels), me * rows, rows, axis=0)

        def drift(states, lo, hi):
            pre = jnp.einsum("krc,cd->krd", states.astype(jnp.bfloat16), w_in, preferred_element_type=jnp.float32)
            outs = []
            for gain, shift in zip(gains, shifts):
                act = jax.nn.gelu(pre * gain[lo:hi, None, :] + shift[lo:hi, None, :]).astype(jnp.bfloat16)
                outs.append(jnp.einsum("krd,dc->krc", act, w_out, preferred_element_type=jnp.float32))
            return h_all[lo:hi, None, None] * ((1.0 + guide) * outs[0] - guide * outs[1])

        drifts = drift(x_rows[None], 0, steps - 1)
        for index in range(1, NUM_SWEEPS):
            running = jnp.cumsum(drifts, axis=0)
            states = x_rows[None] + running[index - 1:steps - 2]
            drifts = jnp.concatenate([drifts[:index], drift(states, index, steps - 1)], axis=0)
        running = jnp.cumsum(drifts, axis=0)
        final = jnp.concatenate([x_rows[None], x_rows[None] + running], axis=0)
        final = lax.all_to_all(final, "time", split_axis=0, concat_axis=1, tiled=True)
        return final.reshape(own_steps, samples, tokens, channels)

    return jax.shard_map(local, mesh=mesh, in_specs=(P("data", None, None), P(None, None), P(None, None), P("time", None), P("time", None), P("time", None), P("time", None), P("time"), P(None)), out_specs=P("time", "data", None, None), check_vma=False)
```

time: 2480 us -> 702 us (0.28)
  waiting for transfers between devices: 1770 us -> 0.06 us
  blocking collectives: 0 us -> 172 us
  starting transfers between devices: 128 us -> 0.01 us
  other arithmetic: 120 us -> 34.4 us
    ppermute x20 -> x0, waiting for transfers between devices: 1770 us -> none  [sweep(): prefix = prefix + lax.ppermute(prefix, 'time', perm)]
    ppermute x20 -> x0, starting transfers between devices: 128 us -> none  [sweep(): prefix = prefix + lax.ppermute(prefix, 'time', perm)]
    all_to_all x0 -> x1, blocking collectives: none -> 122 us  [local(): lax.all_to_all(final, 'time', split_axis=0, concat_axis=1, tiled=True)]
    add x21 -> x1, other arithmetic: 56.2 us -> 2.02 us  [local(): gains = (1.0 + mods[:, 0], 1.0 + mods[:, 2])]
    unnamed x0 -> x1, blocking collectives: none -> 50 us
    sub x4 -> x0, other arithmetic: 31.9 us -> none  [sweep(): before = prefix - dev_total]
    dot_general x8 -> x12, matrix products: 439 us -> 436 us  [the longest x8 333 us: drift(): jnp.einsum('krd,dc->krc', act, w_out, preferred_element_type=jnp.float32)]
  transfers between devices with their start and end apart: 20 -> 1, of which waited for: 20 -> 0; matrix products, arithmetic and copies ran while one was open for 0% -> 2% of each run, Pallas kernels for 0% -> 0%
where the time goes in v1:
time: 702 us; the launch traced here: 695 us
  matrix products  436 us (62%)
  blocking collectives  172 us (25%)
  local copies, waits for them, and re-layouts  37.8 us (5%)
  other arithmetic  34.4 us (5%)
  between operations  14.7 us (2%)
    dot_general x8, matrix products, drift(): jnp.einsum('krd,dc->krc', act, w_out, preferred_element_type=jnp.float32)  333 us
    all_to_all x1, blocking collectives, local(): lax.all_to_all(final, 'time', split_axis=0, concat_axis=1, tiled=True)  122 us
    dot_general x4, matrix products, drift(): jnp.einsum('krc,cd->krd', states.astype(jnp.bfloat16), w_in, preferred_el...  103 us
    unnamed x1, blocking collectives  50 us
    another operation x4, other arithmetic, local(): running = jnp.cumsum(drifts, axis=0)  21.6 us
    unnamed x50, local copies, waits for them, and re-layouts  15.3 us
  transfers between devices with their start and end apart: 1, of which 0 were waited for; matrix products, arithmetic and copies ran while one was open for 2% of the time, Pallas kernels for 0%

profile of v1, /device:TPU:97, one launch (start us, length us, event | category | flops | bytes accessed | tf_op | source)
XLA Modules:
  0.0 695.4 jit_solution(2824231897725260720)
XLA Ops:
  9.1 50.0 %all-reduce = f32[64]{0:T(128)S(1)} all-reduce(f32[64]{0:T(128)S(1)} %dynamic-update-slice), channel_id=1, replica_groups=mesh['data'=1,'time'=32] {'time'}, use_global_device_ids=true, to_apply=%add | all-reduce | flops 64 | bytes 512
  64.1 5.9 fusion.143
  70.0 2.0 convert_element_type.41
  72.0 2.0 slice_add_fusion.4
  81.1 2.0 fusion.185
  84.6 41.0 %fusion.64 = f32[63,32,1152]{2,1,0:T(8,128)} fusion(f32[63,4608]{1,0:T(8,128)} %get-tuple-element.15, f32[63,4608]{1,0:T(8,128)} %bitcast.100, f32[32,4608]{1,0:T(8,128)S(1)} %fusion.143, bf16[4608,1152]{1,0:T(8,128)(2,1)} %param.11), kind=kOutput, calls=%fused_computation.72 | convolution fusion | flops 21505720320 | bytes 22818816 | tf_op jit(solution)/shard_map/krd,dc->krc/dot_general | solution.py:34
  125.6 39.3 %subtract_multiply_fusion = f32[63,32,1152]{2,1,0:T(8,128)S(1)} fusion(f32[63,32,1152]{2,1,0:T(8,128)} %fusion.64, bf16[4608,1152]{1,0:T(8,128)(2,1)} %param.11, f32[63,4608]{1,0:T(8,128)} %get-tuple-element.16, f32[63,4608]{1,0:T(8,128)} %bitcast.98, f32[32,4608]{1,0:T(8,128)S(1)} %fusion.143, f32[]{:T(128)} %bitcast.88, f32[]{:T(128)S(6)} %add.179, ...), kind=kOutput, calls=%fused_computation.119 | convolution fusion | flops 21515010048 | bytes 32108804 | tf_op jit(solution)/shard_map/krd,dc->krc/dot_general | solution.py:34
  165.6 4.3 fusion.186
  172.2 32.8 %fusion.98 = f32[62,32,4608]{2,1,0:T(8,128)} fusion(bf16[1152,4608]{1,0:T(8,128)(2,1)} %param.10, f32[63,32,1152]{2,1,0:T(8,128)} %fusion.186, f32[32,1152]{1,0:T(8,128)S(1)} %constant_dynamic-slice_fusion), kind=kOutput, calls=%fused_computation.102 | convolution fusion | flops 21068365824 | bytes 56475648 | tf_op jit(solution)/shard_map/krc,cd->krd/dot_general | solution.py:30
  205.1 2.0 fusion.184
  208.2 42.0 %fusion.82 = f32[62,32,1152]{2,1,0:T(8,128)} fusion(f32[62,32,4608]{2,1,0:T(8,128)} %fusion.98, f32[62,4608]{1,0:T(8,128)} %get-tuple-element.17, f32[62,4608]{1,0:T(8,128)} %bitcast.96, bf16[4608,1152]{1,0:T(8,128)(2,1)} %param.11), kind=kOutput, calls=%fused_computation.88 | convolution fusion | flops 21164359680 | bytes 58613760 | tf_op jit(solution)/shard_map/krd,dc->krc/dot_general | solution.py:34
  250.2 43.6 %subtract_multiply_fusion.1 = f32[62,32,1152]{2,1,0:T(8,128)} fusion(f32[62,32,1152]{2,1,0:T(8,128)} %fusion.82, bf16[4608,1152]{1,0:T(8,128)(2,1)} %param.11, f32[62,32,4608]{2,1,0:T(8,128)} %fusion.98, f32[62,4608]{1,0:T(8,128)S(1)} %get-tuple-element.18, f32[62,4608]{1,0:T(8,128)} %bitcast.94, f32[]{:T(128)} %bitcast.89, f32[]{:T(128)S(6)} %add.179, ...), kind=kOutput, calls=%fused_computation.122 | convolution fusion | flops 21173501952 | bytes 67756288 | tf_op jit(solution)/shard_map/krd,dc->krc/dot_general | solution.py:34
  297.6 4.1 fusion.109
  303.9 32.5 %fusion.96 = f32[61,32,4608]{2,1,0:T(8,128)} fusion(bf16[1152,4608]{1,0:T(8,128)(2,1)} %param.10, f32[63,32,1152]{2,1,0:T(8,128)} %fusion.109, f32[32,1152]{1,0:T(8,128)S(1)} %constant_dynamic-slice_fusion), kind=kOutput, calls=%fused_computation.100 | convolution fusion | flops 20728553472 | bytes 55738368 | tf_op jit(solution)/shard_map/krc,cd->krd/dot_general | solution.py:30
  339.9 42.3 %fusion.86 = f32[61,32,1152]{2,1,0:T(8,128)} fusion(f32[61,32,4608]{2,1,0:T(8,128)} %fusion.96, f32[61,4608]{1,0:T(8,128)} %get-tuple-element.19, f32[61,4608]{1,0:T(8,128)} %bitcast.99, bf16[4608,1152]{1,0:T(8,128)(2,1)} %param.11), kind=kOutput, calls=%fused_computation.90 | convolution fusion | flops 20822999040 | bytes 57839616 | tf_op jit(solution)/shard_map/krd,dc->krc/dot_general | solution.py:34
  382.3 43.6 %subtract_multiply_fusion.2 = f32[61,32,1152]{2,1,0:T(8,128)} fusion(f32[61,32,1152]{2,1,0:T(8,128)} %fusion.86, bf16[4608,1152]{1,0:T(8,128)(2,1)} %param.11, f32[61,32,4608]{2,1,0:T(8,128)} %fusion.96, f32[61,4608]{1,0:T(8,128)} %get-tuple-element.20, f32[61,4608]{1,0:T(8,128)S(1)} %bitcast.97, f32[]{:T(128)} %bitcast.90, f32[]{:T(128)S(6)} %add.179, ...), kind=kOutput, calls=%fused_computation.125 | convolution fusion | flops 20831993856 | bytes 66834684 | tf_op jit(solution)/shard_map/krd,dc->krc/dot_general | solution.py:34
  427.6 6.6 fusion.108
  435.5 31.5 %fusion.94 = f32[60,32,4608]{2,1,0:T(8,128)} fusion(bf16[1152,4608]{1,0:T(8,128)(2,1)} %param.10, f32[63,32,1152]{2,1,0:T(8,128)} %fusion.108, f32[32,1152]{1,0:T(8,128)S(1)} %constant_dynamic-slice_fusion), kind=kOutput, calls=%fused_computation.98 | convolution fusion | flops 20388741120 | bytes 55001088 | tf_op jit(solution)/shard_map/krc,cd->krd/dot_general | solution.py:30
  469.1 40.0 %fusion.90 = f32[60,32,1152]{2,1,0:T(8,128)} fusion(f32[60,32,4608]{2,1,0:T(8,128)} %fusion.94, f32[60,4608]{1,0:T(8,128)S(1)} %get-tuple-element.21, f32[60,4608]{1,0:T(8,128)S(1)} %bitcast.95, bf16[4608,1152]{1,0:T(8,128)(2,1)} %param.11), kind=kOutput, calls=%fused_computation.92 | convolution fusion | flops 20481638400 | bytes 57065472 | tf_op jit(solution)/shard_map/krd,dc->krc/dot_general | solution.py:34
  509.1 41.4 %subtract_multiply_fusion.3 = f32[60,32,1152]{2,1,0:T(8,128)} fusion(f32[60,32,1152]{2,1,0:T(8,128)} %fusion.90, bf16[4608,1152]{1,0:T(8,128)(2,1)} %param.11, f32[60,32,4608]{2,1,0:T(8,128)} %fusion.94, f32[60,4608]{1,0:T(8,128)S(1)} %get-tuple-element.22, f32[60,4608]{1,0:T(8,128)S(1)} %bitcast.93, f32[]{:T(128)} %bitcast.91, f32[]{:T(128)S(6)} %add.179, ...), kind=kOutput, calls=%fused_computation.130 | convolution fusion | flops 20490485760 | bytes 65913080 | tf_op jit(solution)/shard_map/krd,dc->krc/dot_general | solution.py:34
  550.5 6.6 broadcast_add_fusion
  557.2 4.2 pad_maximum_fusion.2
  561.4 122.3 %all_to_all.15 = f32[64,32,1152]{2,1,0:T(8,128)S(1)} all-to-all(f32[64,32,1152]{2,1,0:T(8,128)S(1)} %pad_maximum_fusion.2), channel_id=1, replica_groups=mesh['data'=1,'time'=32] {'time'}, dimensions={0} | all-to-all | bytes 18874368 | tf_op jit(solution)/shard_map/all_to_all | solution.py:44
  683.7 4.3 copy.13
  (73 shorter events, 34.0 us)
Async XLA Ops:
  6.5 63.4 %all-gather.2.cloned.1.call-start = ((), (), s32[]{:S(2)}) async-start(), calls=%async_computation.1 | async-start | bytes 2433024 | tf_op jit(solution)/shard_map/all_gather | solution.py:21
  76.3 4.8 copy-start
  172.2 32.9 %copy-start.1 = (bf16[64,4,4608]{2,1,0:T(4,128)(2,1)S(1)}, bf16[64,4,4608]{2,1,0:T(4,128)(2,1)}, u32[]{:S(2)}) copy-start(bf16[64,4,4608]{2,1,0:T(4,128)(2,1)} %all-gather.2.cloned.1.call-done) | copy-start | bytes 7077892
  208.2 42.0 %copy-start.17 = (f32[62]{0:T(128)S(1)}, f32[62]{0:T(128)}, u32[]{:S(2)}) copy-start(f32[62]{0:T(128)} %slice.136) | copy-start | bytes 748
  250.2 43.6 %copy-start.11 = (f32[1,32,1152]{2,1,0:T(8,128)S(1)}, f32[1,32,1152]{2,1,0:T(8,128)}, u32[]{:S(2)}) copy-start(f32[1,32,1152]{2,1,0:T(8,128)} %slice.168) | copy-start | bytes 442372
  293.8 3.8 copy-start.4
  297.6 4.1 copy-start.5
  297.6 5.2 copy-start.6
  303.9 32.5 %copy-start.2 = (bf16[64,4,4608]{2,1,0:T(4,128)(2,1)S(1)}, bf16[64,4,4608]{2,1,0:T(4,128)(2,1)}, u32[]{:S(2)}) copy-start(bf16[64,4,4608]{2,1,0:T(4,128)(2,1)} %all-gather.2.cloned.1.call-done) | copy-start | bytes 7077892
  339.9 42.3 %copy-start.13 = (f32[61,1,4608]{2,0,1:T(8,128)S(1)}, f32[61,1,4608]{2,0,1:T(8,128)}, u32[]{:S(2)}) copy-start(f32[61,1,4608]{2,0,1:T(8,128)} %copy.49) | copy-start | bytes 3373060
  339.9 42.3 %copy-start.16 = (f32[61]{0:T(128)S(1)}, f32[61]{0:T(128)}, u32[]{:S(2)}) copy-start(f32[61]{0:T(128)} %slice.145) | copy-start | bytes 736
  382.3 43.6 %copy-start.9 = (f32[2,32,1152]{2,1,0:T(8,128)S(1)}, f32[2,32,1152]{2,1,0:T(8,128)}, u32[]{:S(2)}) copy-start(f32[2,32,1152]{2,1,0:T(8,128)} %fusion.142) | copy-start | bytes 884740
  427.6 6.6 copy-start.7
  427.6 7.7 %copy-start.8 = (f32[60,1,4608]{2,1,0:T(1,128)S(1)}, f32[60,1,4608]{2,1,0:T(1,128)}, u32[]{:S(2)}) copy-start(f32[60,1,4608]{2,1,0:T(1,128)} %slice.186) | copy-start | bytes 3317764
  435.5 31.5 %copy-start.3 = (bf16[64,4,4608]{2,1,0:T(4,128)(2,1)S(1)}, bf16[64,4,4608]{2,1,0:T(4,128)(2,1)}, u32[]{:S(2)}) copy-start(bf16[64,4,4608]{2,1,0:T(4,128)(2,1)} %all-gather.2.cloned.1.call-done) | copy-start | bytes 7077892
  469.1 40.1 %copy-start.12 = (f32[60,1,4608]{2,0,1:T(8,128)S(1)}, f32[60,1,4608]{2,0,1:T(8,128)}, u32[]{:S(2)}) copy-start(f32[60,1,4608]{2,0,1:T(8,128)} %copy.47) | copy-start | bytes 3317764
  469.1 40.1 %copy-start.15 = (f32[60]{0:T(128)S(1)}, f32[60]{0:T(128)}, u32[]{:S(2)}) copy-start(f32[60]{0:T(128)} %slice.154) | copy-start | bytes 724
  509.1 41.4 %copy-start.10 = (f32[3,32,1152]{2,1,0:T(8,128)S(1)}, f32[3,32,1152]{2,1,0:T(8,128)}, u32[]{:S(2)}) copy-start(f32[3,32,1152]{2,1,0:T(8,128)} %fusion.141) | copy-start | bytes 1327108
  550.5 6.6 copy-start.14
Sparse Core Ops, SparseCore 0:
  9.4 42.8 all-gather.1

commit v2 on v1

v2 whole, which is shorter than its diff:
```python
import functools
import math

import jax
import jax.numpy as jnp
from jax import lax
from jax.experimental import pallas as pl
from jax.experimental.pallas import tpu as pltpu
from jax.sharding import PartitionSpec as P

NUM_SWEEPS = 4
ROWS = 8
TILE = 256
MESH = pl.DeviceIdType.MESH
LIN = 2.0 * math.sqrt(2.0 / math.pi)
CUB = 8.0 * 0.044715 * math.sqrt(2.0 / math.pi)


def kernel(num_time, chunk, x_hbm, w_in_hbm, w_out_hbm, mods_hbm, h_ref, guide_ref, land, x_v, w_in, w_out, mods, a0, act, acc, xb, f0, out_v, load_sem, send_sem, self_sem, recv_sem):
    me = lax.axis_index("time")
    steps = mods.shape[1]
    own = steps // num_time
    rows, channels = x_v.shape
    hidden = w_in.shape[1]
    groups = rows // ROWS
    inner = steps - 2

    barrier = pltpu.get_barrier_semaphore()

    def signal(i, carry):
        pl.semaphore_signal(barrier, inc=1, device_id={"time": lax.rem(me + i, num_time)}, device_id_type=MESH)
        return carry

    lax.fori_loop(1, num_time, signal, 0)

    def load(src, dst, sem, parts):
        size = dst.shape[0] // parts
        for i in range(parts):
            pltpu.make_async_copy(src.at[pl.ds(i * size, size)], dst.at[pl.ds(i * size, size)], sem).start()

    load(x_hbm.at[pl.ds(me * rows, rows)], x_v, load_sem.at[0], 1)
    load(w_in_hbm, w_in, load_sem.at[1], 8)
    load(mods_hbm, mods, load_sem.at[2], 4)
    load(w_out_hbm, w_out, load_sem.at[3], 8)

    def loaded(dst, sem):
        pltpu.make_async_copy(dst, dst, sem).wait()

    gain_c, gain_u = 1.0 + guide_ref[0], guide_ref[0]

    def clear(j, carry):
        acc[pl.ds(pl.multiple_of(j * ROWS, ROWS), ROWS), :] = jnp.zeros((ROWS, channels), jnp.float32)
        return carry

    lax.fori_loop(0, steps, clear, 0)

    loaded(x_v, load_sem.at[0])
    loaded(w_in, load_sem.at[1])
    x_cast = x_v[...].astype(jnp.bfloat16)

    def first_act(t, carry):
        cols = pl.ds(pl.multiple_of(t * TILE, TILE), TILE)
        a0[:, cols] = jnp.dot(x_cast, w_in[:, cols], preferred_element_type=jnp.float32)
        return carry

    lax.fori_loop(0, hidden // TILE, first_act, 0)
    loaded(mods, load_sem.at[2])
    loaded(w_out, load_sem.at[3])
    pl.semaphore_wait(barrier, num_time - 1)

    def gelu(z):
        return z + z * jnp.tanh(z * (LIN + CUB * (z * z)))

    def activate(pre_of, lo, count, col, sub):
        cols = pl.ds(col, TILE)
        for pair in range(count // 2):
            for e in range(2):
                halves = []
                for q in range(2):
                    j = lo + 2 * pair + q
                    gain = mods[2 * e, pl.ds(j, 1), cols]
                    shift = mods[2 * e + 1, pl.ds(j, 1), cols]
                    halves.append(gelu(pre_of(2 * pair + q) * gain + shift))
                act[e, pl.ds(2 * ROWS * pair, 2 * ROWS), pl.ds(sub * TILE, TILE)] = jnp.concatenate(halves, axis=0).astype(jnp.bfloat16)

    def project(t, lo, count):
        deep = pl.ds(pl.multiple_of(t * chunk, TILE), chunk)
        for n0 in range(0, channels, TILE):
            wide = pl.ds(n0, min(TILE, channels - n0))
            weights = w_out[deep, wide]
            cond = jnp.dot(act[0, pl.ds(0, count * ROWS), :], weights, preferred_element_type=jnp.float32)
            unc = jnp.dot(act[1, pl.ds(0, count * ROWS), :], weights, preferred_element_type=jnp.float32)
            acc[pl.ds(lo * ROWS, count * ROWS), wide] += gain_c * cond - gain_u * unc

    def take_drift(j):
        where = pl.ds(j * ROWS, ROWS)
        drift = h_ref[j] * acc[where, :]
        acc[where, :] = jnp.zeros((ROWS, channels), jnp.float32)
        return drift

    def to_states(x_g):
        total = f0[...]
        for pair in range(inner // 2):
            first = x_g + total
            total = total + take_drift(1 + 2 * pair)
            second = x_g + total
            total = total + take_drift(2 + 2 * pair)
            xb[pl.ds(2 * ROWS * pair, 2 * ROWS), :] = jnp.concatenate([first, second], axis=0).astype(jnp.bfloat16)

    def to_output(x_g, slot):
        out_v[slot, 0] = x_g
        total = f0[...]
        for j in range(1, steps):
            out_v[slot, j] = x_g + total
            if j < steps - 1:
                total = total + take_drift(j)

    def sent_wait(slot):
        pltpu.make_async_copy(out_v.at[slot, pl.ds(0, steps - own)], out_v.at[slot, pl.ds(0, steps - own)], send_sem.at[slot]).wait()
        pltpu.make_async_copy(out_v.at[slot, pl.ds(0, own)], out_v.at[slot, pl.ds(0, own)], self_sem.at[slot]).wait()

    def group(g, carry):
        mine = pl.ds(pl.multiple_of(g * ROWS, ROWS), ROWS)
        slot = lax.rem(g, 2)
        x_g = x_v[mine, :]

        def first_chunk(t, c):
            for sub in range(chunk // TILE):
                col = pl.multiple_of(t * chunk + sub * TILE, TILE)
                pre = a0[mine, pl.ds(col, TILE)]
                activate(lambda i, pre=pre: pre, 0, steps, col, sub)
            project(t, 0, steps)
            return c

        lax.fori_loop(0, hidden // chunk, first_chunk, 0)
        f0[...] = take_drift(0)
        to_states(x_g)

        def sweep(k, c):
            def one_chunk(t, c2):
                for sub in range(chunk // TILE):
                    col = pl.multiple_of(t * chunk + sub * TILE, TILE)
                    pre = jnp.dot(xb[...], w_in[:, pl.ds(col, TILE)], preferred_element_type=jnp.float32)
                    activate(lambda i, pre=pre: pre[i * ROWS:(i + 1) * ROWS, :], 1, inner, col, sub)
                project(t, 1, inner)
                return c2

            lax.fori_loop(0, hidden // chunk, one_chunk, 0)

            @pl.when(k < NUM_SWEEPS - 1)
            def _():
                to_states(x_g)

            @pl.when(k == NUM_SWEEPS - 1)
            def _():
                @pl.when(g >= 2)
                def _():
                    sent_wait(slot)

                to_output(x_g, slot)

            return c

        lax.fori_loop(1, NUM_SWEEPS, sweep, 0)

        acc[pl.ds((steps - 1) * ROWS, ROWS), :] = jnp.zeros((ROWS, channels), jnp.float32)

        there = pl.ds(pl.multiple_of(me * rows + g * ROWS, ROWS), ROWS)
        pltpu.make_async_copy(out_v.at[slot, pl.ds(me * own, own)], land.at[:, there, :], self_sem.at[slot]).start()

        def send(i, c):
            dest = lax.rem(me + i, num_time)
            pltpu.make_async_remote_copy(
                src_ref=out_v.at[slot, pl.ds(dest * own, own)],
                dst_ref=land.at[:, there, :],
                send_sem=send_sem.at[slot],
                recv_sem=recv_sem.at[0],
                device_id={"time": dest},
                device_id_type=MESH,
            ).start()
            return c

        lax.fori_loop(1, num_time, send, 0)
        return carry

    lax.fori_loop(0, groups, group, 0)
    for slot in range(min(2, groups)):
        sent_wait(slot)
    arrived = land.at[:, pl.ds(0, land.shape[1] - rows), :]
    pltpu.make_async_copy(arrived, arrived, recv_sem.at[0]).wait()


def solution(mesh):
    num_time = mesh.shape["time"]

    def local(x_init, w_in, w_out, gamma_c, beta_c, gamma_u, beta_u, step_h, guide_w):
        samples, tokens, channels = x_init.shape
        own, hidden = gamma_c.shape
        steps = own * num_time
        total_rows = samples * tokens
        rows = total_rows // num_time
        chunk = hidden // 3 if hidden % (3 * TILE) == 0 else hidden // 2

        mods = jnp.stack([gamma_c, beta_c, gamma_u, beta_u], axis=1)
        mods = lax.all_gather(mods, "time", axis=0, tiled=True).astype(jnp.float32)
        one = jnp.asarray([1.0, 0.0, 1.0, 0.0], jnp.float32)
        mods = jnp.swapaxes(0.5 * (mods + one[None, :, None]), 0, 1)
        h_all = lax.all_gather(step_h, "time", axis=0, tiled=True)

        hbm = pl.BlockSpec(memory_space=pl.ANY)
        smem = pl.BlockSpec(memory_space=pltpu.SMEM)
        f32, bf16 = jnp.float32, jnp.bfloat16
        out = pl.pallas_call(
            functools.partial(kernel, num_time, chunk),
            out_shape=jax.ShapeDtypeStruct((own, total_rows, channels), f32),
            in_specs=[hbm, hbm, hbm, hbm, smem, smem],
            out_specs=hbm,
            scratch_shapes=[
                pltpu.VMEM((rows, channels), f32),
                pltpu.VMEM((channels, hidden), bf16),
                pltpu.VMEM((hidden, channels), bf16),
                pltpu.VMEM((4, steps, hidden), f32),
                pltpu.VMEM((rows, hidden), f32),
                pltpu.VMEM((2, steps * ROWS, chunk), bf16),
                pltpu.VMEM((steps * ROWS, channels), f32),
                pltpu.VMEM(((steps - 2) * ROWS, channels), bf16),
                pltpu.VMEM((ROWS, channels), f32),
                pltpu.VMEM((2, steps, ROWS, channels), f32),
                pltpu.SemaphoreType.DMA((4,)),
                pltpu.SemaphoreType.DMA((2,)),
                pltpu.SemaphoreType.DMA((2,)),
                pltpu.SemaphoreType.DMA((1,)),
            ],
            compiler_params=pltpu.CompilerParams(collective_id=0, has_side_effects=True, vmem_limit_bytes=63 * 1024 * 1024),
        )(x_init.reshape(total_rows, channels), w_in, w_out, mods, h_all, guide_w)
        return out.reshape(own, samples, tokens, channels)

    return jax.shard_map(local, mesh=mesh, in_specs=(P("data", None, None), P(None, None), P(None, None), P("time", None), P("time", None), P("time", None), P("time", None), P("time"), P(None)), out_specs=P("time", "data", None, None), check_vma=False)
```

time: 702 us -> 469 us (0.67)
  matrix products: 436 us -> 0 us
  Pallas kernels: 0 us -> 389 us
  blocking collectives: 172 us -> 49.8 us
  other arithmetic: 34.4 us -> 5.5 us
  local copies, waits for them, and re-layouts: 37.8 us -> 9.62 us
    dot_general x12 -> x0, matrix products: 436 us -> none  [the longest x8 333 us: drift(): jnp.einsum('krd,dc->krc', act, w_out, preferred_element_type=jnp.float32)]
    pallas_call x0 -> x1, Pallas kernels: none -> 389 us  [local(): pl.pallas_call(functools.partial(kernel, num_time, chunk), out_shape=jax....]
    all_to_all x1 -> x0, blocking collectives: 122 us -> none  [local(): lax.all_to_all(final, 'time', split_axis=0, concat_axis=1, tiled=True)]
    another operation x4 -> x0, other arithmetic: 21.6 us -> none  [local(): running = jnp.cumsum(drifts, axis=0)]
    slice x16 -> x0, local copies, waits for them, and re-layouts: 15 us -> none  [the longest x4 7.78 us: drift(): shift[lo:hi, None, :]]
    concatenate x3 -> x0, other arithmetic: 7.79 us -> none  [the longest x1 4.25 us: local(): final = jnp.concatenate([x_rows[None], x_rows[None] + running], axis=0)]
    unnamed x50 -> x3, local copies, waits for them, and re-layouts: 15.3 us -> 8.96 us
  transfers between devices with their start and end apart: 1 -> 1, of which waited for: 0 -> 0; matrix products, arithmetic and copies ran while one was open for 2% -> 0% of each run, Pallas kernels for 0% -> 0%
where the time goes in v2:
time: 469 us; the launch traced here: 468 us
  Pallas kernels  389 us (83%)
  blocking collectives  49.8 us (11%)
  between operations  14.1 us (3%)
  local copies, waits for them, and re-layouts  9.62 us (2%)
  other arithmetic  5.5 us (1%)
    pallas_call x1, Pallas kernels, local(): pl.pallas_call(functools.partial(kernel, num_time, chunk), out_shape=jax....  389 us
    unnamed x1, blocking collectives  49.8 us
  transfers between devices with their start and end apart: 1, of which 0 were waited for; matrix products, arithmetic and copies ran while one was open for 0% of the time, Pallas kernels for 0%

profile of v2, /device:TPU:97, one launch (start us, length us, event | category | flops | bytes accessed | tf_op | source)
XLA Modules:
  0.0 468.4 jit_solution(2384875936098814350)
XLA Ops:
  6.5 0.0 all-gather.2.cloned.1.call-start
  6.6 0.9 pad_maximum_fusion
  7.5 0.7 copy.12
  8.1 0.1 all-gather.2.cloned.1.call-update
  8.8 0.9 dynamic-update-slice
  9.7 49.8 %all-reduce.h_ref = f32[64]{0:T(128)} all-reduce(f32[64]{0:T(128)S(1)} %dynamic-update-slice), channel_id=1, replica_groups=mesh['data'=1,'time'=32] {'time'}, use_global_device_ids=true, to_apply=%add | all-reduce | flops 64 | bytes 512
  59.5 0.0 all-gather.2.cloned.1.call-done
  59.5 4.6 multiply_bitcast_fusion.mods_hbm
  64.1 389.3 %shard_map.100 = f32[2,1024,1152]{2,1,0:T(8,128)} custom-call(f32[1024,1152]{1,0:T(8,128)} %bitcast.9, bf16[1152,4608]{1,0:T(8,128)(2,1)} %w_in_hbm.1, bf16[4608,1152]{1,0:T(8,128)(2,1)} %w_out_hbm.1, f32[4,64,4608]{2,1,0:T(8,128)} %multiply_bitcast_fusion.mods_hbm, f32[64]{0:T(128)} %all-reduce.h_ref, f32[1]{0:T(128)S(6)} %copy.17.guide_ref), custom_call_target="tpu_custom_call" | custom-call | tf_op jit(solution)/shard_map/pallas_call | solution.py:213
  453.5 8.1 %copy.18 = f32[2,4,256,1152]{3,2,1,0:T(8,128)} copy(f32[2,4,256,1152]{3,2,1,0:T(8,128)} %bitcast.8) | data formatting | bytes 18874368
  (1 shorter events, 0.0 us)
Async XLA Ops:
  6.5 53.0 %all-gather.2.cloned.1.call-start = ((), (), s32[]{:S(2)}) async-start(), calls=%async_computation | async-start | bytes 2433024 | tf_op jit(solution)/shard_map/all_gather | solution.py:205
Sparse Core Ops, SparseCore 0:
  9.4 42.9 all-gather.1

commit v3 on v2

v3 whole, which is shorter than its diff:
```python
import functools
import math

import jax
import jax.numpy as jnp
from jax import lax
from jax.experimental import pallas as pl
from jax.experimental.pallas import tpu as pltpu
from jax.sharding import PartitionSpec as P

NUM_SWEEPS = 4
ROWS = 8
TILE = 256
MESH = pl.DeviceIdType.MESH
LIN = 2.0 * math.sqrt(2.0 / math.pi)
CUB = 8.0 * 0.044715 * math.sqrt(2.0 / math.pi)


def kernel(num_time, chunk, x_hbm, w_in_hbm, w_out_hbm, mods_src, h_src, guide_ref, land, x_v, w_in, w_out, gathered, mods, h_all, a0, act, acc, xb, f0, out_v, load_sem, give_sem, take_sem, send_sem, self_sem, recv_sem):
    me = lax.axis_index("time")
    own = h_src.shape[0]
    steps = own * num_time
    rows, channels = x_v.shape
    hidden = w_in.shape[1]
    groups = rows // ROWS
    num_chunks = hidden // chunk
    inner = steps - 2
    stride = 7 if math.gcd(7 * 15, num_time) == 1 else 1

    barrier = pltpu.get_barrier_semaphore()

    def signal(i, carry):
        pl.semaphore_signal(barrier, inc=1, device_id={"time": lax.rem(me + i, num_time)}, device_id_type=MESH)
        return carry

    lax.fori_loop(1, num_time, signal, 0)

    def to_peers(send):
        def one(i, carry):
            dest = lax.rem(me + stride * (i + 2 * me), num_time)

            @pl.when(dest != me)
            def _():
                send(dest)

            return carry

        lax.fori_loop(0, num_time, one, 0)

    def remote(src, dst, send, recv, dest):
        return pltpu.make_async_remote_copy(src_ref=src, dst_ref=dst, send_sem=send, recv_sem=recv, device_id={"time": dest}, device_id_type=MESH)

    def load(src, dst, sem, parts):
        size = dst.shape[0] // parts
        for i in range(parts):
            pltpu.make_async_copy(src.at[pl.ds(i * size, size)], dst.at[pl.ds(i * size, size)], sem).start()

    def settle(ref, sem):
        pltpu.make_async_copy(ref, ref, sem).wait()

    load(x_hbm.at[pl.ds(me * rows, rows)], x_v, load_sem.at[0], 1)
    load(w_in_hbm, w_in, load_sem.at[1], 8)
    load(w_out_hbm, w_out, load_sem.at[2], 8)

    pl.semaphore_wait(barrier, num_time - 1)
    for t in range(num_chunks):
        to_peers(lambda dest, t=t: remote(mods_src.at[t], gathered.at[t, me], give_sem.at[0], take_sem.at[t], dest).start())
    to_peers(lambda dest: remote(h_src, h_all.at[me], give_sem.at[1], take_sem.at[num_chunks], dest).start())
    for t in range(num_chunks):
        gathered[t, me] = mods_src[t]
    h_all[me] = h_src[...]

    gain_c, gain_u = 1.0 + guide_ref[0], guide_ref[0]

    def clear(j, carry):
        for g in range(groups):
            acc[g, pl.ds(pl.multiple_of(j * ROWS, ROWS), ROWS), :] = jnp.zeros((ROWS, channels), jnp.float32)
        return carry

    lax.fori_loop(0, steps, clear, 0)

    settle(x_v, load_sem.at[0])
    settle(w_in, load_sem.at[1])
    x_cast = x_v[...].astype(jnp.bfloat16)

    def first_act(t, carry):
        cols = pl.ds(pl.multiple_of(t * 2 * TILE, 2 * TILE), 2 * TILE)
        a0[:, cols] = jnp.dot(x_cast, w_in[:, cols], preferred_element_type=jnp.float32)
        return carry

    lax.fori_loop(0, hidden // (2 * TILE), first_act, 0)
    settle(w_out, load_sem.at[2])

    def gelu(z):
        return z + z * jnp.tanh(z * (LIN + CUB * (z * z)))

    def activate(pre_of, lo, count, col, sub):
        cols = pl.ds(col, TILE)
        for pair in range(count // 2):
            for e in range(2):
                halves = []
                for q in range(2):
                    j = lo + 2 * pair + q
                    gain = mods[j // own, pl.ds(2 * e * own + j % own, 1), cols]
                    shift = mods[j // own, pl.ds((2 * e + 1) * own + j % own, 1), cols]
                    halves.append(gelu(pre_of(2 * pair + q) * gain + shift))
                act[e, pl.ds(2 * ROWS * pair, 2 * ROWS), pl.ds(sub * TILE, TILE)] = jnp.concatenate(halves, axis=0).astype(jnp.bfloat16)

    def project(g, t, lo, count):
        deep = pl.ds(pl.multiple_of(t * chunk, TILE), chunk)
        for n0 in range(0, channels, TILE):
            wide = pl.ds(n0, min(TILE, channels - n0))
            weights = w_out[deep, wide]
            cond = jnp.dot(act[0, pl.ds(0, count * ROWS), :], weights, preferred_element_type=jnp.float32)
            unc = jnp.dot(act[1, pl.ds(0, count * ROWS), :], weights, preferred_element_type=jnp.float32)
            acc[g, pl.ds(lo * ROWS, count * ROWS), wide] += gain_c * cond - gain_u * unc

    def take_drift(g, j):
        where = pl.ds(j * ROWS, ROWS)
        h = jnp.concatenate([h_all[j // own, j % own]] * (channels // 128), axis=1)
        drift = h * acc[g, where, :]
        acc[g, where, :] = jnp.zeros((ROWS, channels), jnp.float32)
        return drift

    def to_states(g, x_g):
        total = f0[...]
        for pair in range(inner // 2):
            first = x_g + total
            total = total + take_drift(g, 1 + 2 * pair)
            second = x_g + total
            total = total + take_drift(g, 2 + 2 * pair)
            xb[pl.ds(2 * ROWS * pair, 2 * ROWS), :] = jnp.concatenate([first, second], axis=0).astype(jnp.bfloat16)

    def to_output(g, x_g, slot):
        out_v[slot, 0] = x_g
        total = f0[...]
        for j in range(1, steps):
            out_v[slot, j] = x_g + total
            if j < steps - 1:
                total = total + take_drift(g, j)

    def sent_wait(slot):
        settle(out_v.at[slot, pl.ds(0, steps - own)], send_sem.at[slot])
        settle(out_v.at[slot, pl.ds(0, own)], self_sem.at[slot])

    row_kind = lax.broadcasted_iota(jnp.int32, (4 * own, chunk), 0) // own
    half = jnp.where(row_kind % 2 == 0, 0.5, 0.0).astype(jnp.float32)

    def first_chunk(t, carry):
        settle(gathered.at[t, pl.ds(0, num_time - 1)], take_sem.at[t])

        def widen(d, c):
            mods[d, :, pl.ds(pl.multiple_of(t * chunk, TILE), chunk)] = 0.5 * gathered[t, d].astype(jnp.float32) + half
            return c

        lax.fori_loop(0, num_time, widen, 0)

        def first_group(g, c):
            for sub in range(chunk // TILE):
                col = pl.multiple_of(t * chunk + sub * TILE, TILE)
                pre = a0[pl.ds(pl.multiple_of(g * ROWS, ROWS), ROWS), pl.ds(col, TILE)]
                activate(lambda i, pre=pre: pre, 0, steps, col, sub)
            project(g, t, 0, steps)
            return c

        lax.fori_loop(0, groups, first_group, 0)
        return carry

    lax.fori_loop(0, num_chunks, first_chunk, 0)
    settle(h_all.at[pl.ds(0, num_time - 1)], take_sem.at[num_chunks])

    def group(g, carry):
        slot = lax.rem(g, 2)
        x_g = x_v[pl.ds(pl.multiple_of(g * ROWS, ROWS), ROWS), :]
        f0[...] = take_drift(g, 0)
        to_states(g, x_g)

        def sweep(k, c):
            def one_chunk(t, c2):
                for sub in range(chunk // TILE):
                    col = pl.multiple_of(t * chunk + sub * TILE, TILE)
                    pre = jnp.dot(xb[...], w_in[:, pl.ds(col, TILE)], preferred_element_type=jnp.float32)
                    activate(lambda i, pre=pre: pre[i * ROWS:(i + 1) * ROWS, :], 1, inner, col, sub)
                project(g, t, 1, inner)
                return c2

            lax.fori_loop(0, num_chunks, one_chunk, 0)

            @pl.when(k < NUM_SWEEPS - 1)
            def _():
                to_states(g, x_g)

            @pl.when(k == NUM_SWEEPS - 1)
            def _():
                @pl.when(g >= 2)
                def _():
                    sent_wait(slot)

                to_output(g, x_g, slot)

            return c

        lax.fori_loop(1, NUM_SWEEPS, sweep, 0)

        there = pl.ds(pl.multiple_of(me * rows + g * ROWS, ROWS), ROWS)
        pltpu.make_async_copy(out_v.at[slot, pl.ds(me * own, own)], land.at[:, there, :], self_sem.at[slot]).start()
        to_peers(lambda dest: remote(out_v.at[slot, pl.ds(dest * own, own)], land.at[:, there, :], send_sem.at[slot], recv_sem.at[0], dest).start())
        return carry

    lax.fori_loop(0, groups, group, 0)
    settle(gathered.at[:, pl.ds(0, num_time - 1)], give_sem.at[0])
    settle(h_all.at[pl.ds(0, num_time - 1)], give_sem.at[1])
    for slot in range(min(2, groups)):
        sent_wait(slot)
    settle(land.at[:, pl.ds(0, land.shape[1] - rows), :], recv_sem.at[0])


def solution(mesh):
    num_time = mesh.shape["time"]

    def local(x_init, w_in, w_out, gamma_c, beta_c, gamma_u, beta_u, step_h, guide_w):
        samples, tokens, channels = x_init.shape
        own, hidden = gamma_c.shape
        steps = own * num_time
        total_rows = samples * tokens
        rows = total_rows // num_time
        chunk = hidden // 3 if hidden % (3 * TILE) == 0 else hidden // 2

        num_chunks = hidden // chunk
        mods = jnp.stack([gamma_c, beta_c, gamma_u, beta_u], axis=0).reshape(4 * own, num_chunks, chunk)
        mods = jnp.swapaxes(mods, 0, 1)
        h_wide = jnp.broadcast_to(step_h[:, None, None], (own, ROWS, 128))

        hbm = pl.BlockSpec(memory_space=pl.ANY)
        vmem = pl.BlockSpec(memory_space=pltpu.VMEM)
        smem = pl.BlockSpec(memory_space=pltpu.SMEM)
        f32, bf16 = jnp.float32, jnp.bfloat16
        out = pl.pallas_call(
            functools.partial(kernel, num_time, chunk),
            out_shape=jax.ShapeDtypeStruct((own, total_rows, channels), f32),
            in_specs=[hbm, hbm, hbm, vmem, vmem, smem],
            out_specs=hbm,
            scratch_shapes=[
                pltpu.VMEM((rows, channels), f32),
                pltpu.VMEM((channels, hidden), bf16),
                pltpu.VMEM((hidden, channels), bf16),
                pltpu.VMEM((num_chunks, num_time, 4 * own, chunk), bf16),
                pltpu.VMEM((num_time, 4 * own, hidden), f32),
                pltpu.VMEM((num_time, own, ROWS, 128), f32),
                pltpu.VMEM((rows, hidden), f32),
                pltpu.VMEM((2, steps * ROWS, chunk), bf16),
                pltpu.VMEM((rows // ROWS, steps * ROWS, channels), f32),
                pltpu.VMEM(((steps - 2) * ROWS, channels), bf16),
                pltpu.VMEM((ROWS, channels), f32),
                pltpu.VMEM((2, steps, ROWS, channels), f32),
                pltpu.SemaphoreType.DMA((3,)),
                pltpu.SemaphoreType.DMA((2,)),
                pltpu.SemaphoreType.DMA((num_chunks + 1,)),
                pltpu.SemaphoreType.DMA((2,)),
                pltpu.SemaphoreType.DMA((2,)),
                pltpu.SemaphoreType.DMA((1,)),
            ],
            compiler_params=pltpu.CompilerParams(collective_id=0, has_side_effects=True, vmem_limit_bytes=63 * 1024 * 1024),
        )(x_init.reshape(total_rows, channels), w_in, w_out, mods, h_wide, guide_w)
        return out.reshape(own, samples, tokens, channels)

    return jax.shard_map(local, mesh=mesh, in_specs=(P("data", None, None), P(None, None), P(None, None), P("time", None), P("time", None), P("time", None), P("time", None), P("time"), P(None)), out_specs=P("time", "data", None, None), check_vma=False)
```

time: 469 us -> 409 us (0.87)
  blocking collectives: 49.8 us -> 0 us
  between operations: 14.1 us -> 0.67 us
  Pallas kernels: 389 us -> 397 us
    unnamed x1 -> x0, blocking collectives: 49.8 us -> none
    pallas_call x1, Pallas kernels: 389 us -> 397 us  [local(): pl.pallas_call(functools.partial(kernel, num_time, chunk), out_shape=jax....]
  transfers between devices with their start and end apart: 1 -> 0, of which waited for: 0 -> 0; matrix products, arithmetic and copies ran while one was open for 0% -> 0% of each run, Pallas kernels for 0% -> 0%
where the time goes in v3:
time: 409 us; the launch traced here: 408 us
  Pallas kernels  397 us (97%)
  local copies, waits for them, and re-layouts  10.1 us (2%)
    pallas_call x1, Pallas kernels, local(): pl.pallas_call(functools.partial(kernel, num_time, chunk), out_shape=jax....  397 us

profile of v3, /device:TPU:97, one launch (start us, length us, event | category | flops | bytes accessed | tf_op | source)
XLA Modules:
  0.0 408.3 jit_solution(7607303938496402908)
XLA Ops:
  0.7 1.3 broadcast_in_dim.2.h_src
  2.0 0.9 pad_maximum_fusion
  2.9 0.1 reshape.11
  2.9 0.7 copy.12
  3.6 396.5 %shard_map.91 = f32[2,1024,1152]{2,1,0:T(8,128)} custom-call(f32[1024,1152]{1,0:T(8,128)} %bitcast.10, bf16[1152,4608]{1,0:T(8,128)(2,1)} %w_in_hbm.1, bf16[4608,1152]{1,0:T(8,128)(2,1)} %w_out_hbm.1, bf16[3,8,1536]{2,1,0:T(8,128)(2,1)} %bitcast.11, f32[2,8,128]{2,1,0:T(8,128)} %broadcast_in_dim.2.h_src, f32[1]{0:T(128)S(6)} %copy.14.guide_ref), custom_call_target="tpu_custom_call" | custom-call | tf_op jit(solution)/shard_map/pallas_call | solution.py:238
  400.1 8.1 %copy.15 = f32[2,4,256,1152]{3,2,1,0:T(8,128)} copy(f32[2,4,256,1152]{3,2,1,0:T(8,128)} %bitcast.9) | data formatting | bytes 18874368

commit v4 on v3

--- a/solution.py
+++ b/solution.py
@@ -101,9 +101,10 @@
                 halves = []
                 for q in range(2):
                     j = lo + 2 * pair + q
-                    gain = mods[j // own, pl.ds(2 * e * own + j % own, 1), cols]
-                    shift = mods[j // own, pl.ds((2 * e + 1) * own + j % own, 1), cols]
-                    halves.append(gelu(pre_of(2 * pair + q) * gain + shift))
+                    block = mods[j // own, :, cols]
+                    gain = block[2 * e * own + j % own:2 * e * own + j % own + 1, :]
+                    at = (2 * e + 1) * own + j % own
+                    halves.append(gelu(pre_of(2 * pair + q) * gain + block[at:at + 1, :]))
                 act[e, pl.ds(2 * ROWS * pair, 2 * ROWS), pl.ds(sub * TILE, TILE)] = jnp.concatenate(halves, axis=0).astype(jnp.bfloat16)
 
     def project(g, t, lo, count):

time: 409 us -> 410 us (level)
  no operation moved by 1% of the time
where the time goes in v4:
time: 410 us; the launch traced here: 409 us
  Pallas kernels  397 us (97%)
  local copies, waits for them, and re-layouts  10.1 us (2%)
    pallas_call x1, Pallas kernels, local(): pl.pallas_call(functools.partial(kernel, num_time, chunk), out_shape=jax....  397 us

profile of v4, /device:TPU:97, one launch (start us, length us, event | category | flops | bytes accessed | tf_op | source)
XLA Modules:
  0.0 408.6 jit_solution(17253619216815696308)
XLA Ops:
  0.7 1.3 broadcast_in_dim.2.h_src
  2.0 0.9 pad_maximum_fusion
  2.9 0.1 reshape.11
  2.9 0.7 copy.12
  3.6 396.9 %shard_map.91 = f32[2,1024,1152]{2,1,0:T(8,128)} custom-call(f32[1024,1152]{1,0:T(8,128)} %bitcast.10, bf16[1152,4608]{1,0:T(8,128)(2,1)} %w_in_hbm.1, bf16[4608,1152]{1,0:T(8,128)(2,1)} %w_out_hbm.1, bf16[3,8,1536]{2,1,0:T(8,128)(2,1)} %bitcast.11, f32[2,8,128]{2,1,0:T(8,128)} %broadcast_in_dim.2.h_src, f32[1]{0:T(128)S(6)} %copy.14.guide_ref), custom_call_target="tpu_custom_call" | custom-call | tf_op jit(solution)/shard_map/pallas_call | solution.py:239
  400.5 8.1 %copy.15 = f32[2,4,256,1152]{3,2,1,0:T(8,128)} copy(f32[2,4,256,1152]{3,2,1,0:T(8,128)} %bitcast.9) | data formatting | bytes 18874368
